TPU v7x, 256 devices: a whole 4x4x8 slice. The times are simulated.
256 devices in a mesh: gx: 16 (over x_lo, y, core), gy: 16 (over x_hi, z).
Axes of the slice: x: 4 (x_hi: 2, x_lo: 2; x = x_hi * 2 + x_lo), y: 4, z: 8, core: 2. Of those that a mesh axis runs over, the one named last changes fastest.
Arguments:
- src_table: bfloat16 [524288, 256], P(('gx', 'gy')), may hold values from -1.5 to 1.5
- src_acc: float32 [524288], P(('gx', 'gy')), may hold values from 0.02 to 0.5
- dst_table: bfloat16 [524288, 256], P(('gx', 'gy')), may hold values from -1.5 to 1.5
- dst_acc: float32 [524288], P(('gx', 'gy')), may hold values from 0.02 to 0.5
- relations: float32 [16, 256], replicated, may hold values from -4 to 4
- rel_acc: float32 [16], replicated, may hold values from 20 to 200
- edge_src: int32 [16, 16, 2, 512], P('gx', 'gy'), may hold values from 0 to 2047
- edge_dst: int32 [16, 16, 2, 512], P('gx', 'gy'), may hold values from 0 to 2047
- edge_rel: int32 [16, 16, 2, 512], P('gx', 'gy'), may hold values from 0 to 15
- negatives: int32 [16, 16, 2, 1, 512], P('gx', 'gy'), may hold values from 0 to 2047
- counts: int32 [16, 16, 2], P('gx', 'gy'), may hold values from 128 to 512
Outputs:
- src_out: bfloat16 [524288, 256], P(('gx', 'gy'))
- src_acc_out: float32 [524288], P(('gx', 'gy'))
- dst_out: bfloat16 [524288, 256], P(('gx', 'gy'))
- dst_acc_out: float32 [524288], P(('gx', 'gy'))
- relations_out: float32 [16, 256], replicated
Inputs may be any that keep to these rules, and one draw needn't show every extreme that they name: `edge_src`: row of the source partition of the bucket. `edge_dst`: row of the destination partition of the bucket. `negatives`: row of the destination partition of the bucket. Only the first counts slots of a bucket's edge lists are live.
All inputs are finite; a program needn't handle non-finite values.
Results may differ from a plain program's by a relative error of at most 0.0027.
Values may be sent and summed in bfloat16 or wider, within the bound.
A program may use at most 64 MiB of HBM per device.

v0:
```python
import functools

import jax
import jax.numpy as jnp
from jax import lax
from jax.experimental import pallas as pl
from jax.experimental.pallas import tpu as pltpu
from jax.sharding import PartitionSpec as P

MESH = pl.DeviceIdType.MESH
bf16, f32, i32 = jnp.bfloat16, jnp.float32, jnp.int32

learn_rate = 0.1
relation_rate = 0.5
CHUNKS = 4
BLOCK = 256
LANES = 128
SRC, DST, REL, NEGS = 0, 1, 2, 3
NT = (((1,), (1,)), ((), ()))
TN = (((0,), (0,)), ((), ()))


def mm(a, b, dims=(((1,), (0,)), ((), ()))):
    return lax.dot_general(a, b, dims, preferred_element_type=f32)


def ones_where(mask):
    return jnp.where(mask, 1.0, 0.0).astype(bf16)


def kernel(
    shape,
    src_hbm, src_acc, dst_hbm, dst_acc, relations, rel_acc, edge_src, edge_dst, edge_rel, negatives, counts,
    src_out, src_acc_out, dst_out, dst_acc_out, rel_out,
    src_tab, dst_tab, src_state, dst_state,
    pack_mine, pack_run, pack_own, cols,
    rel_parts, source, targets, edge_grads, dest_vals, rotated_half, slopes, up_source,
    send_rows, recv_rows, home_grads,
    rel_sum, part, row_buf, col_buf, all_buf, rel_total,
    load_sem, out_sem, idx_send, idx_recv, row_send, row_recv, ret_send, ret_recv, red_send, red_recv,
):
    nx, ny = shape
    rows, width = src_tab.shape
    edges = edge_src.shape[1]
    negs = negatives.shape[1]
    rels = relations.shape[0]
    chunk = edges // CHUNKS
    blocks = rows // BLOCK
    weight = negs ** (-0.5)
    gx, gy = lax.axis_index("gx"), lax.axis_index("gy")

    def peer(dx, dy):
        return (lax.rem(gx + (dx % nx), nx), lax.rem(gy + (dy % ny), ny))

    load_src = pltpu.make_async_copy(src_hbm, src_tab, load_sem.at[0])
    load_dst = pltpu.make_async_copy(dst_hbm, dst_tab, load_sem.at[1])
    load_src.start()
    load_dst.start()

    barrier = pltpu.get_barrier_semaphore()
    partners = [peer(k, 0) for k in range(1, nx)] + [peer(0, k) for k in range(1, ny)]
    partners += [peer(1, -1), peer(-1, 1)]
    for device in partners:
        pl.semaphore_signal(barrier, inc=1, device_id=device, device_id_type=MESH)

    lane = lax.broadcasted_iota(i32, (1, edges), 1)
    for t in range(2):
        pack_mine[4 * t + SRC : 4 * t + SRC + 1, :] = edge_src[t : t + 1, :]
        pack_mine[4 * t + DST : 4 * t + DST + 1, :] = edge_dst[t : t + 1, :]
        pack_mine[4 * t + REL : 4 * t + REL + 1, :] = jnp.where(lane < counts[t], edge_rel[t : t + 1, :], -1)
        pack_mine[4 * t + NEGS : 4 * t + NEGS + 1, :] = negatives[t : t + 1, :]

    rel = relations[...]
    rel_hi = rel.astype(bf16)
    rest = rel - rel_hi.astype(f32)
    rel_mid = rest.astype(bf16)
    rel_low = (rest - rel_mid.astype(f32)).astype(bf16)
    rel_parts[...] = jnp.zeros_like(rel_parts)
    rel_parts[0:rels, :] = rel_hi
    rel_parts[rels : 2 * rels, :] = rel_mid
    rel_parts[2 * rels : 3 * rels, :] = rel_low

    def gather(ids, table):
        spots = lax.broadcasted_iota(i32, (ids.shape[0], rows), 1)
        return mm(ones_where(ids == spots), table[...]).astype(bf16)

    def bucket_chunk(c, from_rows, col):
        at = pl.ds(c * chunk, chunk)
        s = from_rows[at, :].astype(f32)
        d = targets[at, :].astype(f32)
        kind = cols[at, col + REL : col + REL + 1]
        spots = lax.broadcasted_iota(i32, (chunk, rel_parts.shape[0]), 1)
        diagonal = mm(ones_where((spots & (rels - 1)) == kind), rel_parts[...])
        rotated = s * diagonal
        half = rotated.astype(bf16)
        positive = jnp.sum(rotated * d, axis=1, keepdims=True)
        live = jnp.where(kind >= 0, 0.5, 0.0)
        samples = targets[edges:, :]
        scores = mm(half, samples, NT)
        slope = ((live * weight) * (1.0 + jnp.tanh(0.5 * scores))).astype(bf16)
        pulls = -live * (1.0 - jnp.tanh(0.5 * positive))
        upstream = pulls * d + mm(slope, samples)
        edge_grads[at, :] = (upstream * diagonal).astype(bf16)
        dest_vals[at, :] = (pulls * rotated).astype(bf16)
        rotated_half[at, :] = half
        slopes[at, :] = slope
        product = upstream * s
        high = product.astype(bf16)
        up_source[at, 0:width] = high
        up_source[at, width:] = (product - high.astype(f32)).astype(bf16)

    def relation_grad(pack, row):
        kinds = lax.broadcasted_iota(i32, (rels, edges), 0)
        both = mm(ones_where(kinds == pack[row + REL : row + REL + 1, :]), up_source[...])
        return both[:, 0:width] + both[:, width:]

    def negative_grads():
        dest_vals[edges:, :] = mm(slopes[...], rotated_half[...], TN).astype(bf16)

    eye = lax.broadcasted_iota(i32, (LANES, LANES), 0) == lax.broadcasted_iota(i32, (LANES, LANES), 1)

    def update(table, acc_in, acc_new, terms, out=None, sems=None):
        def step(b, carry):
            first = pl.multiple_of(b * BLOCK, BLOCK)
            grad = None
            for ids, values in terms:
                spots = lax.broadcasted_iota(i32, (BLOCK, ids.shape[1]), 0) + first
                term = mm(ones_where(spots == ids), values())
                grad = term if grad is None else grad + term
            for h in range(BLOCK // LANES):
                g = grad[h * LANES : (h + 1) * LANES, :]
                line = pl.ds(b * (BLOCK // LANES) + h, 1)
                squares = g * g
                both = squares[:, 0:LANES] + squares[:, LANES:]
                mixed = both * (1.0 / width) + jnp.where(eye, acc_in[line, :], 0.0)
                state = jnp.sum(mixed, axis=1, keepdims=True)
                acc_new[line, :] = jnp.sum(jnp.where(eye, state, 0.0), axis=0, keepdims=True)
                at = pl.ds(first + h * LANES, LANES)
                moved = table[at, :].astype(f32) - g * (learn_rate * lax.rsqrt(state))
                table[at, :] = moved.astype(bf16)
            if out is not None:
                here = pl.ds(first, BLOCK)
                pltpu.make_async_copy(table.at[here, :], out.at[here, :], sems.at[b]).start()
            return carry

        lax.fori_loop(0, blocks, step, 0)

    def finish(table, out, sems):
        for b in range(blocks):
            here = pl.ds(b * BLOCK, BLOCK)
            pltpu.make_async_copy(table.at[here, :], out.at[here, :], sems.at[b]).wait()

    cols[...] = pack_mine[...].T
    load_src.wait()
    source[...] = gather(cols[:, SRC : SRC + 1], src_tab)
    load_dst.wait()
    targets[0:edges, :] = gather(cols[:, DST : DST + 1], dst_tab)
    targets[edges:, :] = gather(cols[:, NEGS : NEGS + 1], dst_tab)
    for c in range(CHUNKS):
        bucket_chunk(c, source, 0)
    rel_sum[...] = relation_grad(pack_mine, 0)

    pl.semaphore_wait(barrier, len(partners))
    to_run = pltpu.make_async_remote_copy(
        src_ref=pack_mine, dst_ref=pack_run, send_sem=idx_send.at[0], recv_sem=idx_recv.at[0],
        device_id=peer(0, -1), device_id_type=MESH,
    )
    to_own = pltpu.make_async_remote_copy(
        src_ref=pack_mine, dst_ref=pack_own, send_sem=idx_send.at[1], recv_sem=idx_recv.at[1],
        device_id=peer(-1, 0), device_id_type=MESH,
    )
    to_own.start()
    to_run.start()

    update(src_tab, src_acc, src_state, [(pack_mine[SRC : SRC + 1, :], lambda: edge_grads[...])])

    to_own.wait()
    cols[...] = pack_own[...].T

    def row_copy(c):
        at = pl.ds(c * chunk, chunk)
        return pltpu.make_async_remote_copy(
            src_ref=send_rows.at[at, :], dst_ref=recv_rows.at[at, :], send_sem=row_send.at[c], recv_sem=row_recv.at[c],
            device_id=peer(1, -1), device_id_type=MESH,
        )

    def home_copy(c):
        at = pl.ds(c * chunk, chunk)
        return pltpu.make_async_remote_copy(
            src_ref=edge_grads.at[at, :], dst_ref=home_grads.at[at, :], send_sem=ret_send.at[c], recv_sem=ret_recv.at[c],
            device_id=peer(-1, 1), device_id_type=MESH,
        )

    for c in range(0, CHUNKS, 2):
        both = gather(cols[c * chunk : (c + 2) * chunk, 4 + SRC : 5 + SRC], src_tab)
        send_rows[c * chunk : (c + 2) * chunk, :] = both
        row_copy(c).start()
        row_copy(c + 1).start()

    negative_grads()
    dest_terms = lambda pack, row: [
        (pack[row + DST : row + DST + 1, :], lambda: dest_vals[0:edges, :]),
        (pack[row + NEGS : row + NEGS + 1, :], lambda: dest_vals[edges:, :]),
    ]
    update(dst_tab, dst_acc, dst_state, dest_terms(pack_mine, 0))
    to_run.wait()
    cols[...] = pack_run[...].T
    targets[0:edges, :] = gather(cols[:, 4 + DST : 5 + DST], dst_tab)
    targets[edges:, :] = gather(cols[:, 4 + NEGS : 5 + NEGS], dst_tab)

    for c in range(CHUNKS):
        row_copy(c).wait()
        bucket_chunk(c, recv_rows, 4)
        home_copy(c).start()
    total = rel_sum[...] + relation_grad(pack_run, 4)
    for i in range(rels):
        part[i] = total[i : i + 1, :]

    def scatter_copy(k):
        to = lax.rem(gx + k, nx)
        return pltpu.make_async_remote_copy(
            src_ref=part.at[to], dst_ref=row_buf.at[gx], send_sem=red_send.at[0, k], recv_sem=red_recv.at[0, k],
            device_id=(to, gy), device_id_type=MESH,
        )

    def cross_copy(k):
        to = lax.rem(gy + k, ny)
        return pltpu.make_async_remote_copy(
            src_ref=col_buf.at[gy], dst_ref=col_buf.at[gy], send_sem=red_send.at[1, k], recv_sem=red_recv.at[1, k],
            device_id=(gx, to), device_id_type=MESH,
        )

    def spread_copy(k):
        to = lax.rem(gx + k, nx)
        return pltpu.make_async_remote_copy(
            src_ref=all_buf.at[gx], dst_ref=all_buf.at[gx], send_sem=red_send.at[2, k], recv_sem=red_recv.at[2, k],
            device_id=(to, gy), device_id_type=MESH,
        )

    for k in range(1, nx):
        scatter_copy(k).start()
    row_buf[gx] = part[gx]

    negative_grads()
    update(dst_tab, dst_state, dst_acc_out, dest_terms(pack_run, 4), dst_out, out_sem.at[0])

    for k in range(1, nx):
        scatter_copy(k).wait()
    row = row_buf[0]
    for i in range(1, nx):
        row = row + row_buf[i]
    col_buf[gy] = row
    for k in range(1, ny):
        cross_copy(k).start()

    for c in range(CHUNKS):
        home_copy(c).wait()
    update(
        src_tab, src_state, src_acc_out, [(pack_own[4 + SRC : 5 + SRC, :], lambda: home_grads[...])], src_out, out_sem.at[1]
    )

    for k in range(1, ny):
        cross_copy(k).wait()
    row = col_buf[0]
    for i in range(1, ny):
        row = row + col_buf[i]
    all_buf[gx] = row
    for k in range(1, nx):
        spread_copy(k).start()
    finish(dst_tab, dst_out, out_sem.at[0])
    finish(src_tab, src_out, out_sem.at[1])
    for k in range(1, nx):
        spread_copy(k).wait()
    for i in range(rels):
        rel_total[i : i + 1, :] = all_buf[i]
    grad = rel_total[...]
    corner = lax.broadcasted_iota(i32, (rels, rels), 0) == lax.broadcasted_iota(i32, (rels, rels), 1)
    state = jnp.sum(jnp.where(corner, rel_acc[...], 0.0), axis=1, keepdims=True)
    state = state + jnp.sum(grad * grad, axis=1, keepdims=True) * (1.0 / width)
    rel_out[...] = relations[...] - relation_rate * grad * lax.rsqrt(state)


def solution(mesh):
    nx, ny = mesh.shape["gx"], mesh.shape["gy"]

    def local(src_table, src_acc, dst_table, dst_acc, relations, rel_acc, edge_src, edge_dst, edge_rel, negatives, counts):
        rows, width = src_table.shape
        edges = edge_src.shape[-1]
        negs = negatives.shape[-1]
        rels = relations.shape[0]
        lines = rows // LANES
        vmem = pl.BlockSpec(memory_space=pltpu.VMEM)
        smem = pl.BlockSpec(memory_space=pltpu.SMEM)
        hbm = pl.BlockSpec(memory_space=pl.ANY)
        table = jax.ShapeDtypeStruct((rows, width), bf16)
        state = jax.ShapeDtypeStruct((lines, LANES), f32)
        dma = pltpu.SemaphoreType.DMA
        out = pl.pallas_call(
            functools.partial(kernel, (nx, ny)),
            out_shape=(table, state, table, state, jax.ShapeDtypeStruct((rels, width), f32)),
            in_specs=[hbm, vmem, hbm, vmem, vmem, vmem, vmem, vmem, vmem, vmem, smem],
            out_specs=(hbm, vmem, hbm, vmem, vmem),
            scratch_shapes=[
                pltpu.VMEM((rows, width), bf16),
                pltpu.VMEM((rows, width), bf16),
                pltpu.VMEM((lines, LANES), f32),
                pltpu.VMEM((lines, LANES), f32),
                pltpu.VMEM((8, edges), i32),
                pltpu.VMEM((8, edges), i32),
                pltpu.VMEM((8, edges), i32),
                pltpu.VMEM((edges, 8), i32),
                pltpu.VMEM((LANES, width), bf16),
                pltpu.VMEM((edges, width), bf16),
                pltpu.VMEM((edges + negs, width), bf16),
                pltpu.VMEM((edges, width), bf16),
                pltpu.VMEM((edges + negs, width), bf16),
                pltpu.VMEM((edges, width), bf16),
                pltpu.VMEM((edges, negs), bf16),
                pltpu.VMEM((edges, 2 * width), bf16),
                pltpu.VMEM((edges, width), bf16),
                pltpu.VMEM((edges, width), bf16),
                pltpu.VMEM((edges, width), bf16),
                pltpu.VMEM((rels, width), f32),
                pltpu.VMEM((rels, 1, width), f32),
                pltpu.VMEM((nx, 1, width), f32),
                pltpu.VMEM((ny, 1, width), f32),
                pltpu.VMEM((nx, 1, width), f32),
                pltpu.VMEM((rels, width), f32),
                dma((2,)),
                dma((2, rows // BLOCK)),
                dma((2,)),
                dma((2,)),
                dma((CHUNKS,)),
                dma((CHUNKS,)),
                dma((CHUNKS,)),
                dma((CHUNKS,)),
                dma((3, max(nx, ny))),
                dma((3, max(nx, ny))),
            ],
            compiler_params=pltpu.CompilerParams(collective_id=0, has_side_effects=True, vmem_limit_bytes=48 << 20),
        )(
            src_table,
            src_acc.reshape(lines, LANES),
            dst_table,
            dst_acc.reshape(lines, LANES),
            relations,
            rel_acc.reshape(1, rels),
            edge_src.reshape(2, edges),
            edge_dst.reshape(2, edges),
            edge_rel.reshape(2, edges),
            negatives.reshape(2, negs),
            counts.reshape(2),
        )
        return (out[0], out[1].reshape(rows), out[2], out[3].reshape(rows), out[4])

    both = ("gx", "gy")
    listed = P("gx", "gy", None, None)
    return jax.shard_map(
        local,
        mesh=mesh,
        in_specs=(
            P(both, None), P(both), P(both, None), P(both), P(), P(),
            listed, listed, listed, P("gx", "gy", None, None, None), P("gx", "gy", None),
        ),
        out_specs=(P(both, None), P(both), P(both, None), P(both), P()),
        check_vma=False,
    )
```

profile of v0, /device:TPU:1, one launch (start us, length us, event | category | flops | bytes accessed | tf_op | source)
XLA Modules:
  0.0 52.7 jit_solution(15127254226211029589)
XLA Ops:
  0.6 0.0 copy-start.2
  0.6 0.0 copy-start.5
  0.7 0.7 %copy.18 = s32[1,1,2,1,512]{4,2,3,1,0:T(2,128)S(1)} copy(s32[1,1,2,1,512]{4,3,2,1,0:T(1,128)} %param.20) | data formatting | bytes 8192
  1.4 0.0 copy-start.8
  1.4 0.0 copy-start.9
  1.4 0.0 copy-done.2
  1.4 0.0 copy-done.5
  1.4 0.6 %copy-done.8 = f32[16]{0:T(128)S(1)} copy-done((f32[16]{0:T(128)S(1)}, f32[16]{0:T(128)}, u32[]{:S(2)}) %copy-start.8) | copy-done | bytes 88
  2.0 0.0 copy-done.9
  2.0 0.0 copy-start
  2.0 1.2 %copy-done = bf16[2048,256]{1,0:T(8,128)(2,1)S(1)} copy-done((bf16[2048,256]{1,0:T(8,128)(2,1)S(1)}, bf16[2048,256]{1,0:T(8,128)(2,1)}, u32[]{:S(2)}) %copy-start) | copy-done | bytes 1048600
  3.3 0.0 copy-start.1
  3.3 1.2 %copy-done.1 = bf16[2048,256]{1,0:T(8,128)(2,1)S(1)} copy-done((bf16[2048,256]{1,0:T(8,128)(2,1)S(1)}, bf16[2048,256]{1,0:T(8,128)(2,1)}, u32[]{:S(2)}) %copy-start.1) | copy-done | bytes 1048600
  4.5 0.0 copy-start.3
  4.5 0.7 %copy-done.3 = f32[2048]{0:T(1024)S(1)} copy-done((f32[2048]{0:T(1024)S(1)}, f32[2048]{0:T(1024)}, u32[]{:S(2)}) %copy-start.3) | copy-done | bytes 8216
  5.2 0.0 copy-start.4
  5.2 0.7 %copy-done.4 = f32[2048]{0:T(1024)S(1)} copy-done((f32[2048]{0:T(1024)S(1)}, f32[2048]{0:T(1024)}, u32[]{:S(2)}) %copy-start.4) | copy-done | bytes 8216
  5.9 0.0 copy-start.6
  5.9 0.7 %copy-done.6 = s32[1,1,2,512]{3,2,1,0:T(2,128)S(1)} copy-done((s32[1,1,2,512]{3,2,1,0:T(2,128)S(1)}, s32[1,1,2,512]{3,2,1,0:T(2,128)}, u32[]{:S(2)}) %copy-start.6) | copy-done | bytes 4120
  6.6 0.0 copy-start.7
  6.6 0.7 %copy-done.7 = s32[1,1,2,512]{3,2,1,0:T(2,128)S(1)} copy-done((s32[1,1,2,512]{3,2,1,0:T(2,128)S(1)}, s32[1,1,2,512]{3,2,1,0:T(2,128)}, u32[]{:S(2)}) %copy-start.7) | copy-done | bytes 4120
  7.2 41.7 %shard_map.146 = (bf16[2048,256]{1,0:T(8,128)(2,1)S(1)}, f32[16,128]{1,0:T(8,128)S(1)}, bf16[2048,256]{1,0:T(8,128)(2,1)S(1)}, f32[16,128]{1,0:T(8,128)S(1)}, f32[16,256]{1,0:T(8,128)S(1)}) custom-call(bf16[2048,256]{1,0:T(8,128)(2,1)S(1)} %copy-done, f32[16,128]{1,0:T(8,128)S(1)} %bitcast.13, bf16[2048,256]{1,0:T(8,128)(2,1)S(1)} %copy-done.1, ...), custom_call_target="tpu_custom_call" | custom-call | tf_op jit(solution)/shard_map/pallas_call | solution.py:298
  48.9 1.0 %copy.24 = bf16[2048,256]{1,0:T(8,128)(2,1)} copy(bf16[2048,256]{1,0:T(8,128)(2,1)S(1)} %get-tuple-element.20) | data formatting | bytes 2097152
  49.9 0.6 %copy.25 = f32[2048]{0:T(1024)} copy(f32[2048]{0:T(1024)S(1)} %bitcast.16) | data formatting | bytes 16384
  50.5 1.0 %copy.26 = bf16[2048,256]{1,0:T(8,128)(2,1)} copy(bf16[2048,256]{1,0:T(8,128)(2,1)S(1)} %get-tuple-element.22) | data formatting | bytes 2097152
  51.5 0.6 %copy.27 = f32[2048]{0:T(1024)} copy(f32[2048]{0:T(1024)S(1)} %bitcast.15) | data formatting | bytes 16384
  52.1 0.6 %copy.28 = f32[16,256]{1,0:T(8,128)} copy(f32[16,256]{1,0:T(8,128)S(1)} %get-tuple-element.24) | data formatting | bytes 32768
Async XLA Ops:
  0.6 0.7 %copy-start.2 = (f32[16,256]{1,0:T(8,128)S(1)}, f32[16,256]{1,0:T(8,128)}, u32[]{:S(2)}) copy-start(f32[16,256]{1,0:T(8,128)} %relations.1) | copy-start | bytes 49156
  0.6 0.7 %copy-start.5 = (s32[1,1,2,512]{3,2,1,0:T(2,128)S(1)}, s32[1,1,2,512]{3,2,1,0:T(2,128)}, u32[]{:S(2)}) copy-start(s32[1,1,2,512]{3,2,1,0:T(2,128)} %param.17) | copy-start | bytes 12292
  1.4 0.7 %copy-start.8 = (f32[16]{0:T(128)S(1)}, f32[16]{0:T(128)}, u32[]{:S(2)}) copy-start(f32[16]{0:T(128)} %param.16) | copy-start | bytes 196
  1.4 0.7 %copy-start.9 = (s32[1,1,2]{2,1,0:T(1,128)S(1)}, s32[1,1,2]{2,1,0:T(1,128)}, u32[]{:S(2)}) copy-start(s32[1,1,2]{2,1,0:T(1,128)} %param.21) | copy-start | bytes 28
  2.0 1.2 %copy-start = (bf16[2048,256]{1,0:T(8,128)(2,1)S(1)}, bf16[2048,256]{1,0:T(8,128)(2,1)}, u32[]{:S(2)}) copy-start(bf16[2048,256]{1,0:T(8,128)(2,1)} %src_hbm.1) | copy-start | bytes 3145732
  3.3 1.2 %copy-start.1 = (bf16[2048,256]{1,0:T(8,128)(2,1)S(1)}, bf16[2048,256]{1,0:T(8,128)(2,1)}, u32[]{:S(2)}) copy-start(bf16[2048,256]{1,0:T(8,128)(2,1)} %dst_hbm.1) | copy-start | bytes 3145732
  4.5 0.7 %copy-start.3 = (f32[2048]{0:T(1024)S(1)}, f32[2048]{0:T(1024)}, u32[]{:S(2)}) copy-start(f32[2048]{0:T(1024)} %param.12) | copy-start | bytes 24580
  5.2 0.7 %copy-start.4 = (f32[2048]{0:T(1024)S(1)}, f32[2048]{0:T(1024)}, u32[]{:S(2)}) copy-start(f32[2048]{0:T(1024)} %param.14) | copy-start | bytes 24580
  5.9 0.7 %copy-start.6 = (s32[1,1,2,512]{3,2,1,0:T(2,128)S(1)}, s32[1,1,2,512]{3,2,1,0:T(2,128)}, u32[]{:S(2)}) copy-start(s32[1,1,2,512]{3,2,1,0:T(2,128)} %param.18) | copy-start | bytes 12292
  6.6 0.7 %copy-start.7 = (s32[1,1,2,512]{3,2,1,0:T(2,128)S(1)}, s32[1,1,2,512]{3,2,1,0:T(2,128)}, u32[]{:S(2)}) copy-start(s32[1,1,2,512]{3,2,1,0:T(2,128)} %param.19) | copy-start | bytes 12292
where the time goes:
time: 53.1 us; the launch traced here: 52.7 us
  Pallas kernels  41.7 us (79%)
  local copies, waits for them, and re-layouts  10.3 us (19%)
  between operations  0.68 us (1%)
    pallas_call x1, Pallas kernels, local(): pl.pallas_call(functools.partial(kernel, (nx, ny)), out_shape=(table, sta...  41.7 us
    unnamed x26, local copies, waits for them, and re-layouts  10.3 us

commit v1 on v0

v1 whole, which is shorter than its diff:
```python
import functools

import jax
import jax.numpy as jnp
from jax import lax
from jax.experimental import pallas as pl
from jax.experimental.pallas import tpu as pltpu
from jax.sharding import PartitionSpec as P

MESH = pl.DeviceIdType.MESH
bf16, f32, i32 = jnp.bfloat16, jnp.float32, jnp.int32

learn_rate = 0.1
relation_rate = 0.5
CHUNKS = 4
BLOCK = 256
LANES = 128
SRC, DST, REL, NEGS = 0, 1, 2, 3
NT = (((1,), (1,)), ((), ()))
TN = (((0,), (0,)), ((), ()))


def mm(a, b, dims=(((1,), (0,)), ((), ()))):
    return lax.dot_general(a, b, dims, preferred_element_type=f32)


def ones_where(mask):
    return jnp.where(mask, 1.0, 0.0).astype(bf16)


def kernel(
    shape,
    src_hbm, src_acc_hbm, dst_hbm, dst_acc_hbm, relations_hbm, rel_acc_hbm, edge_src_hbm, edge_dst_hbm, edge_rel_hbm, negatives_hbm,
    counts_hbm,
    src_tab, src_acc_out, dst_tab, dst_acc_out, rel_out,
    src_acc, dst_acc, relations, rel_acc, edge_src, edge_dst, edge_rel, negatives, counts,
    src_state, dst_state,
    pack_mine, pack_run, pack_own, cols,
    rel_parts, acc_parts, source, targets, edge_grads, dest_vals, rotated_half, slopes, up_source,
    send_rows, recv_rows, run_grads, home_grads,
    rel_sum, part, row_buf, col_buf, all_buf, rel_total,
    load_sem, idx_send, idx_recv, row_send, row_recv, ret_send, ret_recv, red_send, red_recv,
):
    nx, ny = shape
    rows, width = src_tab.shape
    lines = rows // LANES
    edges = edge_src.shape[1]
    rels = relations.shape[0]
    chunk = edges // CHUNKS
    blocks = rows // BLOCK
    weight = negatives.shape[-1] ** (-0.5)
    gx, gy = lax.axis_index("gx"), lax.axis_index("gy")
    half_x, half_y = nx // 2, ny // 2

    def peer(dx, dy):
        return (lax.rem(gx + (dx % nx), nx), lax.rem(gy + (dy % ny), ny))

    def near(k):
        return ((gx // half_x) * half_x + lax.rem(gx + k, half_x), gy)

    def far(offset):
        a, b, c = offset
        x = lax.rem(gx // half_x + a, 2) * half_x + lax.rem(gx, half_x)
        y = lax.rem(gy // half_y + b, 2) * half_y + lax.rem(gy + c, half_y)
        return (x, y)

    offsets = [(a, b, c) for a in range(2) for b in range(2) for c in range(half_y)][1:]
    offsets.sort(key=lambda o: -min(o[2], half_y - o[2]) - (2 if o[:2] == (0, 1) else max(o[:2])))

    def loaded(k, source_ref, target_ref):
        return pltpu.make_async_copy(source_ref, target_ref, load_sem.at[k])

    loads = [
        loaded(k, *pair)
        for k, pair in enumerate(
            (
                (edge_src_hbm, edge_src), (edge_dst_hbm, edge_dst), (edge_rel_hbm, edge_rel), (negatives_hbm, negatives),
                (counts_hbm, counts), (relations_hbm, relations), (src_hbm, src_tab), (dst_hbm, dst_tab),
                (src_acc_hbm, src_acc), (dst_acc_hbm, dst_acc), (rel_acc_hbm, rel_acc),
            )
        )
    ]
    for copy in loads:
        copy.start()

    barrier = pltpu.get_barrier_semaphore()
    partners = [far(o) for o in offsets] + [near(k) for k in range(1, half_x)]
    partners += [peer(1, 0), peer(-1, 0), peer(1, -1), peer(-1, 1)]
    if ny > 2:
        partners += [peer(0, 1), peer(0, -1)]
    for device in partners:
        pl.semaphore_signal(barrier, inc=1, device_id=device, device_id_type=MESH)

    for copy in loads[:6]:
        copy.wait()
    lane = lax.broadcasted_iota(i32, (1, edges), 1)
    for t in range(2):
        pack_mine[4 * t + SRC : 4 * t + SRC + 1, :] = edge_src[t : t + 1, :]
        pack_mine[4 * t + DST : 4 * t + DST + 1, :] = edge_dst[t : t + 1, :]
        pack_mine[4 * t + REL : 4 * t + REL + 1, :] = jnp.where(lane < counts[0:1, t : t + 1], edge_rel[t : t + 1, :], -1)
        pack_mine[4 * t + NEGS : 4 * t + NEGS + 1, :] = negatives[t]

    def split(value, parts):
        count = value.shape[0]
        parts[...] = jnp.zeros_like(parts)
        high = value.astype(bf16)
        rest = value - high.astype(f32)
        middle = rest.astype(bf16)
        parts[0:count, :] = high
        parts[count : 2 * count, :] = middle
        parts[2 * count : 3 * count, :] = (rest - middle.astype(f32)).astype(bf16)

    def pick(ids, parts, count):
        spots = lax.broadcasted_iota(i32, (ids.shape[0], parts.shape[0]), 1)
        return mm(ones_where((spots & (count - 1)) == ids), parts[...])

    split(relations[...], rel_parts)

    def gather(ids, table):
        spots = lax.broadcasted_iota(i32, (ids.shape[0], rows), 1)
        return mm(ones_where(ids == spots), table[...]).astype(bf16)

    def bucket_chunk(c, from_rows, col, grads):
        at = pl.ds(c * chunk, chunk)
        s = from_rows[at, :].astype(f32)
        d = targets[at, :].astype(f32)
        kind = cols[at, col + REL : col + REL + 1]
        diagonal = pick(kind, rel_parts, rels)
        rotated = s * diagonal
        half = rotated.astype(bf16)
        positive = jnp.sum(rotated * d, axis=1, keepdims=True)
        live = jnp.where(kind >= 0, 0.5, 0.0)
        samples = targets[edges:, :]
        scores = mm(half, samples, NT)
        slope = ((live * weight) * (1.0 + jnp.tanh(0.5 * scores))).astype(bf16)
        pulls = -live * (1.0 - jnp.tanh(0.5 * positive))
        upstream = pulls * d + mm(slope, samples)
        grads[at, :] = (upstream * diagonal).astype(bf16)
        dest_vals[at, :] = (pulls * rotated).astype(bf16)
        rotated_half[at, :] = half
        slopes[at, :] = slope
        product = upstream * s
        high = product.astype(bf16)
        up_source[at, 0:width] = high
        up_source[at, width:] = (product - high.astype(f32)).astype(bf16)

    def relation_grad(pack, row):
        kinds = lax.broadcasted_iota(i32, (rels, edges), 0)
        both = mm(ones_where(kinds == pack[row + REL : row + REL + 1, :]), up_source[...])
        return both[:, 0:width] + both[:, width:]

    def negative_grads():
        dest_vals[edges:, :] = mm(slopes[...], rotated_half[...], TN).astype(bf16)

    eye = lax.broadcasted_iota(i32, (LANES, LANES), 0) == lax.broadcasted_iota(i32, (LANES, LANES), 1)

    def update(table, acc_in, acc_new, terms):
        def step(b, carry):
            first = pl.multiple_of(b * BLOCK, BLOCK)
            grad = None
            for ids, values in terms:
                spots = lax.broadcasted_iota(i32, (BLOCK, ids.shape[1]), 0) + first
                term = mm(ones_where(spots == ids), values())
                grad = term if grad is None else grad + term
            for h in range(BLOCK // LANES):
                g = grad[h * LANES : (h + 1) * LANES, :]
                line = pl.ds(b * (BLOCK // LANES) + h, 1)
                squares = g * g
                both = squares[:, 0:LANES] + squares[:, LANES:]
                mixed = both * (1.0 / width) + jnp.where(eye, acc_in[line, :], 0.0)
                state = jnp.sum(mixed, axis=1, keepdims=True)
                acc_new[line, :] = jnp.sum(jnp.where(eye, state, 0.0), axis=0, keepdims=True)
                at = pl.ds(first + h * LANES, LANES)
                moved = table[at, :].astype(f32) - g * (learn_rate * lax.rsqrt(state))
                table[at, :] = moved.astype(bf16)
            return carry

        lax.fori_loop(0, blocks, step, 0, unroll=2)

    cols[...] = pack_mine[...].T
    loads[6].wait()
    source[...] = gather(cols[:, SRC : SRC + 1], src_tab)
    loads[7].wait()
    targets[0:edges, :] = gather(cols[:, DST : DST + 1], dst_tab)
    targets[edges:, :] = gather(cols[:, NEGS : NEGS + 1], dst_tab)
    for copy in loads[8:]:
        copy.wait()
    split(src_acc[...], acc_parts)

    pl.semaphore_wait(barrier, len(partners))
    to_own = pltpu.make_async_remote_copy(
        src_ref=pack_mine, dst_ref=pack_own, send_sem=idx_send.at[1], recv_sem=idx_recv.at[1],
        device_id=peer(-1, 0), device_id_type=MESH,
    )
    to_run = pltpu.make_async_remote_copy(
        src_ref=pack_mine, dst_ref=pack_run, send_sem=idx_send.at[0], recv_sem=idx_recv.at[0],
        device_id=peer(0, -1), device_id_type=MESH,
    )
    to_own.start()
    to_run.start()

    for c in range(CHUNKS):
        bucket_chunk(c, source, 0, edge_grads)

    def row_copy(c):
        at = pl.ds(c * chunk, chunk)
        return pltpu.make_async_remote_copy(
            src_ref=send_rows.at[at, :], dst_ref=recv_rows.at[at, :], send_sem=row_send.at[c], recv_sem=row_recv.at[c],
            device_id=peer(1, -1), device_id_type=MESH,
        )

    def home_copy(c):
        at = pl.ds(c * chunk, chunk)
        return pltpu.make_async_remote_copy(
            src_ref=run_grads.at[at, :], dst_ref=home_grads.at[at, :], send_sem=ret_send.at[c], recv_sem=ret_recv.at[c],
            device_id=peer(-1, 1), device_id_type=MESH,
        )

    to_own.wait()
    cols[...] = pack_own[...].T
    source[...] = gather(cols[:, 4 + SRC : 5 + SRC], src_tab)
    for c in range(CHUNKS):
        at = pl.ds(c * chunk, chunk)
        named = cols[at, 4 + SRC : 5 + SRC]
        g = mm(ones_where(named == pack_mine[SRC : SRC + 1, :]), edge_grads[...])
        squares = g * g
        spots = lax.broadcasted_iota(i32, (chunk, LANES), 1)
        accs = pick(named // LANES, acc_parts, lines)
        mixed = (squares[:, 0:LANES] + squares[:, LANES:]) * (1.0 / width) + jnp.where(spots == lax.rem(named, LANES), accs, 0.0)
        state = jnp.sum(mixed, axis=1, keepdims=True)
        send_rows[at, :] = (source[at, :].astype(f32) - g * (learn_rate * lax.rsqrt(state))).astype(bf16)
        row_copy(c).start()

    rel_sum[...] = relation_grad(pack_mine, 0)
    update(src_tab, src_acc, src_state, [(pack_mine[SRC : SRC + 1, :], lambda: edge_grads[...])])
    negative_grads()
    dest_terms = lambda pack, row: [
        (pack[row + DST : row + DST + 1, :], lambda: dest_vals[0:edges, :]),
        (pack[row + NEGS : row + NEGS + 1, :], lambda: dest_vals[edges:, :]),
    ]
    update(dst_tab, dst_acc, dst_state, dest_terms(pack_mine, 0))
    to_run.wait()
    cols[...] = pack_run[...].T
    targets[0:edges, :] = gather(cols[:, 4 + DST : 5 + DST], dst_tab)
    targets[edges:, :] = gather(cols[:, 4 + NEGS : 5 + NEGS], dst_tab)

    for c in range(CHUNKS):
        row_copy(c).wait()
        bucket_chunk(c, recv_rows, 4, run_grads)
        home_copy(c).start()
    total = rel_sum[...] + relation_grad(pack_run, 4)
    each = rels // half_x
    for i in range(half_x):
        part[i] = total[i * each : (i + 1) * each, :]

    place = lax.rem(gx, half_x)
    mine = (gx // half_x) * ny + gy

    def scatter_copy(k):
        device = near(k)
        return pltpu.make_async_remote_copy(
            src_ref=part.at[lax.rem(device[0], half_x)], dst_ref=row_buf.at[place],
            send_sem=red_send.at[0, k], recv_sem=red_recv.at[0, k], device_id=device, device_id_type=MESH,
        )

    def cross_copy(k):
        return pltpu.make_async_remote_copy(
            src_ref=col_buf.at[mine], dst_ref=col_buf.at[mine],
            send_sem=red_send.at[1, k], recv_sem=red_recv.at[1, k], device_id=far(offsets[k]), device_id_type=MESH,
        )

    def spread_copy(k):
        return pltpu.make_async_remote_copy(
            src_ref=all_buf.at[place], dst_ref=all_buf.at[place],
            send_sem=red_send.at[2, k], recv_sem=red_recv.at[2, k], device_id=near(k), device_id_type=MESH,
        )

    nears, fars = range(1, half_x), range(len(offsets))
    for k in nears:
        scatter_copy(k).start()
    row_buf[place] = part[place]
    negative_grads()
    for k in nears:
        scatter_copy(k).wait()
    row = row_buf[0]
    for i in range(1, half_x):
        row = row + row_buf[i]
    col_buf[mine] = row
    for k in fars:
        cross_copy(k).start()

    update(dst_tab, dst_state, dst_acc_out, dest_terms(pack_run, 4))

    for c in range(CHUNKS):
        home_copy(c).wait()
    update(src_tab, src_state, src_acc_out, [(pack_own[4 + SRC : 5 + SRC, :], lambda: home_grads[...])])

    for k in fars:
        cross_copy(k).wait()
    row = col_buf[0]
    for i in range(1, 2 * ny):
        row = row + col_buf[i]
    all_buf[place] = row
    for k in nears:
        spread_copy(k).start()
    for k in nears:
        spread_copy(k).wait()
    for i in range(half_x):
        rel_total[i * each : (i + 1) * each, :] = all_buf[i]
    grad = rel_total[...]
    corner = lax.broadcasted_iota(i32, (rels, rels), 0) == lax.broadcasted_iota(i32, (rels, rels), 1)
    state = jnp.sum(jnp.where(corner, rel_acc[...], 0.0), axis=1, keepdims=True)
    state = state + jnp.sum(grad * grad, axis=1, keepdims=True) * (1.0 / width)
    rel_out[...] = relations[...] - relation_rate * grad * lax.rsqrt(state)


def store(*refs):
    count = len(refs) // 2
    sems = refs[-1]
    copies = [pltpu.make_async_copy(refs[i], refs[count + i], sems.at[i]) for i in range(count)]
    for copy in copies:
        copy.start()
    for copy in copies:
        copy.wait()


def solution(mesh):
    nx, ny = mesh.shape["gx"], mesh.shape["gy"]

    def local(src_table, src_acc, dst_table, dst_acc, relations, rel_acc, edge_src, edge_dst, edge_rel, negatives, counts):
        rows, width = src_table.shape
        edges = edge_src.shape[-1]
        negs = negatives.shape[-1]
        rels = relations.shape[0]
        lines = rows // LANES
        vmem = pl.BlockSpec(memory_space=pltpu.VMEM)
        hbm = pl.BlockSpec(memory_space=pltpu.HBM)
        table = jax.ShapeDtypeStruct((rows, width), bf16)
        state = jax.ShapeDtypeStruct((lines, LANES), f32)
        outs = (table, state, table, state, jax.ShapeDtypeStruct((rels, width), f32))
        dma = pltpu.SemaphoreType.DMA
        half, far, each = nx // 2, 2 * ny, rels // (nx // 2)
        inner = pl.pallas_call(
            functools.partial(kernel, (nx, ny)),
            out_shape=outs,
            in_specs=[hbm] * 11,
            out_specs=(vmem,) * 5,
            scratch_shapes=[
                pltpu.VMEM((lines, LANES), f32),
                pltpu.VMEM((lines, LANES), f32),
                pltpu.VMEM((rels, width), f32),
                pltpu.VMEM((1, rels), f32),
                pltpu.VMEM((2, edges), i32),
                pltpu.VMEM((2, edges), i32),
                pltpu.VMEM((2, edges), i32),
                pltpu.VMEM((2, 1, negs), i32),
                pltpu.VMEM((1, 2), i32),
                pltpu.VMEM((lines, LANES), f32),
                pltpu.VMEM((lines, LANES), f32),
                pltpu.VMEM((8, edges), i32),
                pltpu.VMEM((8, edges), i32),
                pltpu.VMEM((8, edges), i32),
                pltpu.VMEM((edges, 8), i32),
                pltpu.VMEM((LANES, width), bf16),
                pltpu.VMEM((LANES, LANES), bf16),
                pltpu.VMEM((edges, width), bf16),
                pltpu.VMEM((edges + negs, width), bf16),
                pltpu.VMEM((edges, width), bf16),
                pltpu.VMEM((edges + negs, width), bf16),
                pltpu.VMEM((edges, width), bf16),
                pltpu.VMEM((edges, negs), bf16),
                pltpu.VMEM((edges, 2 * width), bf16),
                pltpu.VMEM((edges, width), bf16),
                pltpu.VMEM((edges, width), bf16),
                pltpu.VMEM((edges, width), bf16),
                pltpu.VMEM((edges, width), bf16),
                pltpu.VMEM((rels, width), f32),
                pltpu.VMEM((half, each, width), f32),
                pltpu.VMEM((half, each, width), f32),
                pltpu.VMEM((far, each, width), f32),
                pltpu.VMEM((half, each, width), f32),
                pltpu.VMEM((rels, width), f32),
                dma((11,)),
                dma((2,)),
                dma((2,)),
                dma((CHUNKS,)),
                dma((CHUNKS,)),
                dma((CHUNKS,)),
                dma((CHUNKS,)),
                dma((3, far)),
                dma((3, far)),
            ],
            compiler_params=pltpu.CompilerParams(collective_id=0, has_side_effects=True, vmem_limit_bytes=40 << 20),
        )(
            *(
                pltpu.with_memory_space_constraint(value, pltpu.HBM)
                for value in (
                    src_table,
                    src_acc.reshape(lines, LANES),
                    dst_table,
                    dst_acc.reshape(lines, LANES),
                    relations,
                    rel_acc.reshape(1, rels),
                    edge_src.reshape(2, edges),
                    edge_dst.reshape(2, edges),
                    edge_rel.reshape(2, edges),
                    negatives.reshape(2, 1, negs),
                    counts.reshape(1, 2),
                )
            )
        )
        out = pl.pallas_call(
            store,
            out_shape=outs,
            in_specs=[vmem] * 5,
            out_specs=(hbm,) * 5,
            scratch_shapes=[dma((5,))],
            compiler_params=pltpu.CompilerParams(vmem_limit_bytes=1 << 20),
        )(*inner)
        return (out[0], out[1].reshape(rows), out[2], out[3].reshape(rows), out[4])

    both = ("gx", "gy")
    listed = P("gx", "gy", None, None)
    return jax.shard_map(
        local,
        mesh=mesh,
        in_specs=(
            P(both, None), P(both), P(both, None), P(both), P(), P(),
            listed, listed, listed, P("gx", "gy", None, None, None), P("gx", "gy", None),
        ),
        out_specs=(P(both, None), P(both), P(both, None), P(both), P()),
        check_vma=False,
    )
```

time: 53.1 us -> 42.9 us (0.81)
  local copies, waits for them, and re-layouts: 10.3 us -> 0 us
    unnamed x26 -> x0, local copies, waits for them, and re-layouts: 10.3 us -> none
    pallas_call x1 -> x2, Pallas kernels: 41.7 us -> 42.2 us  [the longest x1 40.8 us: local(): pl.pallas_call(functools.partial(kernel, (nx, ny)), out_shape=outs, in_sp...]
where the time goes in v1:
time: 42.9 us; the launch traced here: 42.8 us
  Pallas kernels  42.2 us (98%)
  between operations  0.64 us (1%)
    pallas_call x1, Pallas kernels, local(): pl.pallas_call(functools.partial(kernel, (nx, ny)), out_shape=outs, in_sp...  40.8 us
    pallas_call x1, Pallas kernels, local(): pl.pallas_call(store, out_shape=outs, in_specs=[vmem] * 5, out_specs=(hbm...  1.37 us

profile of v1, /device:TPU:1, one launch (start us, length us, event | category | flops | bytes accessed | tf_op | source)
XLA Modules:
  0.0 42.8 jit_solution(14979255382751276957)
XLA Ops:
  0.6 40.8 %shard_map.146 = (bf16[2048,256]{1,0:T(8,128)(2,1)S(1)}, f32[16,128]{1,0:T(8,128)S(1)}, bf16[2048,256]{1,0:T(8,128)(2,1)S(1)}, f32[16,128]{1,0:T(8,128)S(1)}, f32[16,256]{1,0:T(8,128)S(1)}) custom-call(bf16[2048,256]{1,0:T(8,128)(2,1)} %src_hbm.1, f32[16,128]{1,0:T(8,128)} %bitcast.10, bf16[2048,256]{1,0:T(8,128)(2,1)} %dst_hbm.1, f32[16,128]{1,0:T(8,128)} %bitcast.11, ...), custom_call_target="tpu_custom_call" | custom-call | tf_op jit(solution)/shard_map/pallas_call | solution.py:343
  41.5 1.4 %shard_map.147 = (bf16[2048,256]{1,0:T(8,128)(2,1)}, f32[16,128]{1,0:T(8,128)}, bf16[2048,256]{1,0:T(8,128)(2,1)}, f32[16,128]{1,0:T(8,128)}, f32[16,256]{1,0:T(8,128)}) custom-call(bf16[2048,256]{1,0:T(8,128)(2,1)S(1)} %get-tuple-element.15.refs_0_, f32[16,128]{1,0:T(8,128)S(1)} %get-tuple-element.16.refs_1_, ...), custom_call_target="tpu_custom_call" | custom-call | tf_op jit(solution)/shard_map/pallas_call | solution.py:412

commit v2 on v1

--- a/solution.py
+++ b/solution.py
@@ -14,6 +14,8 @@
 relation_rate = 0.5
 CHUNKS = 4
 BLOCK = 256
+UNROLL = 2
+FIRST = 256
 LANES = 128
 SRC, DST, REL, NEGS = 0, 1, 2, 3
 NT = (((1,), (1,)), ((), ()))
@@ -39,7 +41,7 @@
     rel_parts, acc_parts, source, targets, edge_grads, dest_vals, rotated_half, slopes, up_source,
     send_rows, recv_rows, run_grads, home_grads,
     rel_sum, part, row_buf, col_buf, all_buf, rel_total,
-    load_sem, idx_send, idx_recv, row_send, row_recv, ret_send, ret_recv, red_send, red_recv,
+    load_sem, met, idx_send, idx_recv, row_send, row_recv, ret_send, ret_recv, red_send, red_recv,
 ):
     nx, ny = shape
     rows, width = src_tab.shape
@@ -84,12 +86,21 @@
         copy.start()
 
     barrier = pltpu.get_barrier_semaphore()
-    partners = [far(o) for o in offsets] + [near(k) for k in range(1, half_x)]
-    partners += [peer(1, 0), peer(-1, 0), peer(1, -1), peer(-1, 1)]
-    if ny > 2:
-        partners += [peer(0, 1), peer(0, -1)]
+    partners = [peer(1, 0), peer(-1, 0), peer(0, 1), peer(0, -1), peer(1, -1), peer(-1, 1)]
     for device in partners:
         pl.semaphore_signal(barrier, inc=1, device_id=device, device_id_type=MESH)
+
+    def greet(k, devices):
+        for device in devices:
+            pl.semaphore_signal(met.at[k], inc=1, device_id=device, device_id_type=MESH)
+
+    def greet_both(k, step):
+        greet(k, [peer(step, 0), peer(-step, 0)])
+        greet(k + 3, [peer(0, step), peer(0, -step)])
+
+    def met_both(k):
+        pl.semaphore_wait(met.at[k], 2)
+        pl.semaphore_wait(met.at[k + 3], 2)
 
     for copy in loads[:6]:
         copy.wait()
@@ -120,8 +131,8 @@
         spots = lax.broadcasted_iota(i32, (ids.shape[0], rows), 1)
         return mm(ones_where(ids == spots), table[...]).astype(bf16)
 
-    def bucket_chunk(c, from_rows, col, grads):
-        at = pl.ds(c * chunk, chunk)
+    def bucket_chunk(first, count, from_rows, col, grads):
+        at = pl.ds(first, count)
         s = from_rows[at, :].astype(f32)
         d = targets[at, :].astype(f32)
         kind = cols[at, col + REL : col + REL + 1]
@@ -154,7 +165,7 @@
 
     eye = lax.broadcasted_iota(i32, (LANES, LANES), 0) == lax.broadcasted_iota(i32, (LANES, LANES), 1)
 
-    def update(table, acc_in, acc_new, terms):
+    def update(table, acc_in, acc_new, terms, begin=0, end=None):
         def step(b, carry):
             first = pl.multiple_of(b * BLOCK, BLOCK)
             grad = None
@@ -175,17 +186,11 @@
                 table[at, :] = moved.astype(bf16)
             return carry
 
-        lax.fori_loop(0, blocks, step, 0, unroll=2)
+        lax.fori_loop(begin, blocks if end is None else end, step, 0, unroll=UNROLL)
 
     cols[...] = pack_mine[...].T
     loads[6].wait()
     source[...] = gather(cols[:, SRC : SRC + 1], src_tab)
-    loads[7].wait()
-    targets[0:edges, :] = gather(cols[:, DST : DST + 1], dst_tab)
-    targets[edges:, :] = gather(cols[:, NEGS : NEGS + 1], dst_tab)
-    for copy in loads[8:]:
-        copy.wait()
-    split(src_acc[...], acc_parts)
 
     pl.semaphore_wait(barrier, len(partners))
     to_own = pltpu.make_async_remote_copy(
@@ -198,9 +203,18 @@
     )
     to_own.start()
     to_run.start()
-
-    for c in range(CHUNKS):
-        bucket_chunk(c, source, 0, edge_grads)
+    greet_both(0, 1)
+
+    loads[7].wait()
+    targets[0:edges, :] = gather(cols[:, DST : DST + 1], dst_tab)
+    targets[edges:, :] = gather(cols[:, NEGS : NEGS + 1], dst_tab)
+    for copy in loads[8:]:
+        copy.wait()
+    split(src_acc[...], acc_parts)
+    for first in range(0, edges, FIRST):
+        bucket_chunk(first, FIRST, source, 0, edge_grads)
+    met_both(0)
+    greet_both(1, 2)
 
     def row_copy(c):
         at = pl.ds(c * chunk, chunk)
@@ -232,22 +246,30 @@
         row_copy(c).start()
 
     rel_sum[...] = relation_grad(pack_mine, 0)
-    update(src_tab, src_acc, src_state, [(pack_mine[SRC : SRC + 1, :], lambda: edge_grads[...])])
     negative_grads()
+    met_both(1)
+    greet_both(2, 4)
     dest_terms = lambda pack, row: [
         (pack[row + DST : row + DST + 1, :], lambda: dest_vals[0:edges, :]),
         (pack[row + NEGS : row + NEGS + 1, :], lambda: dest_vals[edges:, :]),
     ]
     update(dst_tab, dst_acc, dst_state, dest_terms(pack_mine, 0))
+    met_both(2)
+    greet(6, [peer(half_x, 0)])
     to_run.wait()
     cols[...] = pack_run[...].T
     targets[0:edges, :] = gather(cols[:, 4 + DST : 5 + DST], dst_tab)
     targets[edges:, :] = gather(cols[:, 4 + NEGS : 5 + NEGS], dst_tab)
 
+    cuts = (0, 2, 4, blocks, blocks)
     for c in range(CHUNKS):
         row_copy(c).wait()
-        bucket_chunk(c, recv_rows, 4, run_grads)
+        bucket_chunk(c * chunk, chunk, recv_rows, 4, run_grads)
         home_copy(c).start()
+        if cuts[c] < cuts[c + 1]:
+            terms = [(pack_mine[SRC : SRC + 1, :], lambda: edge_grads[...])]
+            update(src_tab, src_acc, src_state, terms, cuts[c], cuts[c + 1])
+    pl.semaphore_wait(met.at[6], 1)
     total = rel_sum[...] + relation_grad(pack_run, 4)
     each = rels // half_x
     for i in range(half_x):
@@ -256,55 +278,47 @@
     place = lax.rem(gx, half_x)
     mine = (gx // half_x) * ny + gy
 
-    def scatter_copy(k):
+    def exchange(phase, source_ref, target_ref, device):
+        pltpu.make_async_remote_copy(
+            src_ref=source_ref, dst_ref=target_ref, send_sem=red_send.at[phase], recv_sem=red_recv.at[phase],
+            device_id=device, device_id_type=MESH,
+        ).start()
+
+    def all_of(sem, phase, buf, count):
+        ref = buf.at[pl.ds(0, count)]
+        pltpu.make_async_copy(ref, ref, sem.at[phase]).wait()
+
+    def added(buf):
+        terms = [buf[i] for i in range(buf.shape[0])]
+        while len(terms) > 1:
+            terms = [terms[i] + terms[i + 1] for i in range(0, len(terms), 2)]
+        return terms[0]
+
+    nears = half_x - 1
+    for k in range(1, half_x):
         device = near(k)
-        return pltpu.make_async_remote_copy(
-            src_ref=part.at[lax.rem(device[0], half_x)], dst_ref=row_buf.at[place],
-            send_sem=red_send.at[0, k], recv_sem=red_recv.at[0, k], device_id=device, device_id_type=MESH,
-        )
-
-    def cross_copy(k):
-        return pltpu.make_async_remote_copy(
-            src_ref=col_buf.at[mine], dst_ref=col_buf.at[mine],
-            send_sem=red_send.at[1, k], recv_sem=red_recv.at[1, k], device_id=far(offsets[k]), device_id_type=MESH,
-        )
-
-    def spread_copy(k):
-        return pltpu.make_async_remote_copy(
-            src_ref=all_buf.at[place], dst_ref=all_buf.at[place],
-            send_sem=red_send.at[2, k], recv_sem=red_recv.at[2, k], device_id=near(k), device_id_type=MESH,
-        )
-
-    nears, fars = range(1, half_x), range(len(offsets))
-    for k in nears:
-        scatter_copy(k).start()
+        exchange(0, part.at[lax.rem(device[0], half_x)], row_buf.at[place], device)
     row_buf[place] = part[place]
     negative_grads()
-    for k in nears:
-        scatter_copy(k).wait()
-    row = row_buf[0]
-    for i in range(1, half_x):
-        row = row + row_buf[i]
-    col_buf[mine] = row
-    for k in fars:
-        cross_copy(k).start()
-
     update(dst_tab, dst_state, dst_acc_out, dest_terms(pack_run, 4))
+
+    all_of(red_recv, 0, row_buf, nears)
+    col_buf[mine] = added(row_buf)
+    for offset in offsets:
+        exchange(1, col_buf.at[mine], col_buf.at[mine], far(offset))
 
     for c in range(CHUNKS):
         home_copy(c).wait()
     update(src_tab, src_state, src_acc_out, [(pack_own[4 + SRC : 5 + SRC, :], lambda: home_grads[...])])
 
-    for k in fars:
-        cross_copy(k).wait()
-    row = col_buf[0]
-    for i in range(1, 2 * ny):
-        row = row + col_buf[i]
-    all_buf[place] = row
-    for k in nears:
-        spread_copy(k).start()
-    for k in nears:
-        spread_copy(k).wait()
+    all_of(red_recv, 1, col_buf, len(offsets))
+    all_buf[place] = added(col_buf)
+    for k in range(1, half_x):
+        exchange(2, all_buf.at[place], all_buf.at[place], near(k))
+    all_of(red_send, 0, row_buf, nears)
+    all_of(red_send, 1, col_buf, len(offsets))
+    all_of(red_recv, 2, all_buf, nears)
+    all_of(red_send, 2, all_buf, nears)
     for i in range(half_x):
         rel_total[i * each : (i + 1) * each, :] = all_buf[i]
     grad = rel_total[...]
@@ -381,14 +395,15 @@
                 pltpu.VMEM((half, each, width), f32),
                 pltpu.VMEM((rels, width), f32),
                 dma((11,)),
+                pltpu.SemaphoreType.REGULAR((7,)),
                 dma((2,)),
                 dma((2,)),
                 dma((CHUNKS,)),
                 dma((CHUNKS,)),
                 dma((CHUNKS,)),
                 dma((CHUNKS,)),
-                dma((3, far)),
-                dma((3, far)),
+                dma((3,)),
+                dma((3,)),
             ],
             compiler_params=pltpu.CompilerParams(collective_id=0, has_side_effects=True, vmem_limit_bytes=40 << 20),
         )(

time: 42.9 us -> 41.7 us (0.972)
  Pallas kernels: 42.2 us -> 40.9 us
    pallas_call x1, Pallas kernels: 40.8 us -> 39.6 us  [local(): pl.pallas_call(functools.partial(kernel, (nx, ny)), out_shape=outs, in_sp...]
where the time goes in v2:
time: 41.7 us; the launch traced here: 41.6 us
  Pallas kernels  40.9 us (98%)
  between operations  0.64 us (2%)
    pallas_call x1, Pallas kernels, local(): pl.pallas_call(functools.partial(kernel, (nx, ny)), out_shape=outs, in_sp...  39.6 us
    pallas_call x1, Pallas kernels, local(): pl.pallas_call(store, out_shape=outs, in_specs=[vmem] * 5, out_specs=(hbm...  1.37 us

profile of v2, /device:TPU:1, one launch (start us, length us, event | category | flops | bytes accessed | tf_op | source)
XLA Modules:
  0.0 41.6 jit_solution(13272108068380464377)
XLA Ops:
  0.6 39.6 %shard_map.146 = (bf16[2048,256]{1,0:T(8,128)(2,1)S(1)}, f32[16,128]{1,0:T(8,128)S(1)}, bf16[2048,256]{1,0:T(8,128)(2,1)S(1)}, f32[16,128]{1,0:T(8,128)S(1)}, f32[16,256]{1,0:T(8,128)S(1)}) custom-call(bf16[2048,256]{1,0:T(8,128)(2,1)} %src_hbm.1, f32[16,128]{1,0:T(8,128)} %bitcast.10, bf16[2048,256]{1,0:T(8,128)(2,1)} %dst_hbm.1, f32[16,128]{1,0:T(8,128)} %bitcast.11, ...), custom_call_target="tpu_custom_call" | custom-call | tf_op jit(solution)/shard_map/pallas_call | solution.py:357
  40.2 1.4 %shard_map.147 = (bf16[2048,256]{1,0:T(8,128)(2,1)}, f32[16,128]{1,0:T(8,128)}, bf16[2048,256]{1,0:T(8,128)(2,1)}, f32[16,128]{1,0:T(8,128)}, f32[16,256]{1,0:T(8,128)}) custom-call(bf16[2048,256]{1,0:T(8,128)(2,1)S(1)} %get-tuple-element.15.refs_0_, f32[16,128]{1,0:T(8,128)S(1)} %get-tuple-element.16.refs_1_, ...), custom_call_target="tpu_custom_call" | custom-call | tf_op jit(solution)/shard_map/pallas_call | solution.py:427
